TPU v7x, 128 devices: a whole 4x4x4 slice. The times are simulated.
128 devices in a mesh: dp: 16 (over y_hi, x, core), mp: 8 (over y_lo, z).
Axes of the slice: x: 4, y: 4 (y_hi: 2, y_lo: 2; y = y_hi * 2 + y_lo), z: 4, core: 2. Of those that a mesh axis runs over, the one named last changes fastest.
Arguments:
- activations: bfloat16 [16384, 8192], P('dp'), may hold values from -18 to 18
- curvature: float32 [16384, 2048], P('dp', 'mp'), may hold values from 0.05 to 5
- basis: float32 [12, 16777216], P(None, ('dp', 'mp')), may hold values from -6 to 6
- krylov: float32 [16777216], P(('dp', 'mp')), may hold values from -38 to 38
Outputs:
- new_vector: float32 [16777216], P(('dp', 'mp'))
- hessenberg: float32 [13], replicated
All inputs are finite; a program needn't handle non-finite values.
Results may differ from a plain program's by a relative error of at most 0.0058.
Values may be sent and summed in bfloat16 or wider, within the bound.
A program may use at most 128 MiB of HBM per device.

v0:
```python
import functools

import jax
import jax.numpy as jnp
from jax import lax
from jax.sharding import Mesh
from jax.sharding import PartitionSpec as P

KEY_VALUE_HEADS = 8
HD = 128
PARAMS = 16777216
DP = ("dp_0", "dp_1", "dp_2")
MP = ("mp_0", "mp_1")
DP_MP = ("dp_0", "dp_1", "dp_2", "mp_0", "mp_1")


def in_blocks(value, dim, peers):
    shape = value.shape
    tiles = value.reshape(*shape[:dim], peers, shape[dim] // peers, *shape[dim + 1 :])
    return jnp.moveaxis(tiles, dim, 0)


def summed_on_arrival(value, axis, dim):
    tiles = in_blocks(value, dim, lax.axis_size(axis))
    arrived = lax.all_to_all(tiles, axis, split_axis=0, concat_axis=0, tiled=True)
    return arrived.astype(jnp.float32).sum(axis=0)


def over_axes(value, axes):
    return functools.reduce(lax.psum, axes, value)


def body(activations, curvature, basis, krylov):
    data_count = lax.axis_size(DP)
    model_count = lax.axis_size(MP)
    tok_rows = activations.shape[0]
    every_head_stack = KEY_VALUE_HEADS
    head_depth = HD
    local_heads = every_head_stack // model_count
    columns_dev = local_heads * 2 * head_depth
    rows_dev = krylov.shape[0] // (every_head_stack * 2 * head_depth)
    lowered_duplicate = krylov.astype(jnp.bfloat16).reshape(
        rows_dev, every_head_stack, 2, head_depth
    )
    local_rows = lax.all_to_all(
        lowered_duplicate, MP, split_axis=1, concat_axis=0, tiled=True
    ).reshape(rows_dev * model_count, columns_dev)
    columns = activations
    projected_coefficients = jnp.dot(
        columns,
        lax.all_gather(local_rows, DP, axis=0, tiled=True),
        preferred_element_type=jnp.float32,
    )
    weighted = (curvature * projected_coefficients).astype(jnp.bfloat16)
    columns = activations
    scattered = summed_on_arrival(
        lax.dot_general(
            columns, weighted, (((0,), (0,)), ((), ())), preferred_element_type=jnp.float32
        ).astype(jnp.bfloat16),
        DP,
        0,
    )
    owned = lax.all_to_all(
        scattered.reshape(rows_dev * model_count, local_heads, 2, head_depth).astype(jnp.bfloat16),
        MP,
        split_axis=0,
        concat_axis=1,
        tiled=True,
    ).astype(jnp.float32)
    curved = owned.reshape(krylov.shape[0]) / (tok_rows * data_count)
    param_total = float(PARAMS)
    coeffs, squares, gram_matrix = (
        over_axes(jnp.dot(basis, curved, precision=lax.Precision.HIGHEST) / param_total, DP_MP),
        over_axes(jnp.sum(curved * curved) / param_total, DP_MP),
        over_axes(jnp.dot(basis, basis.T, precision=lax.Precision.HIGHEST) / param_total, DP_MP),
    )
    residual_vector = curved - jnp.dot(coeffs, basis, precision=lax.Precision.HIGHEST)
    mean_square = (
        squares
        - 2.0 * jnp.sum(coeffs * coeffs)
        + jnp.sum(coeffs * jnp.dot(gram_matrix, coeffs, precision=lax.Precision.HIGHEST))
    )
    scale_norm = jnp.sqrt(mean_square + 1e-06)
    return (residual_vector / scale_norm, jnp.concatenate([coeffs, scale_norm[None]]))


def solution(mesh):
    finer = Mesh(mesh.devices.reshape(2, 4, 2, 2, 4), ("dp_0", "dp_1", "dp_2", "mp_0", "mp_1"))
    placed = (P(DP, None), P(DP, MP), P(None, DP_MP), P(DP_MP))
    return jax.shard_map(
        body, mesh=finer, in_specs=placed, out_specs=(P(DP_MP), P()), check_vma=False
    )
```

profile of v0, /device:TPU:0, one launch (start us, length us, event | category | flops | bytes accessed | tf_op | source)
XLA Modules:
  0.0 258.6 jit_solution(6615962206934037297)
XLA Ops:
  7.2 0.0 all-gather.2.cloned.1.call-start
  7.2 1.1 convert_element_type.35
  8.3 0.2 copy.11
  8.5 13.5 %all_to_all.29 = bf16[64,8,2,128]{3,2,0,1:T(2,128)(2,1)S(1)} all-to-all(bf16[64,8,2,128]{3,2,0,1:T(2,128)(2,1)S(1)} %copy.11), channel_id=1, replica_groups=mesh['dp_0'=2,'dp_1'=4,'dp_2'=2,'mp_0'=2,'mp_1'=4] {'mp_0','mp_1'}, dimensions={1} | all-to-all | bytes 524288 | tf_op jit(solution)/shard_map/all_to_all | solution.py:45
  21.9 0.7 copy.22
  22.7 0.0 all-gather.2.cloned.1.call-update
  22.7 55.3 %all-gather.2.cloned.1.call-done = bf16[8192,256]{1,0:T(8,128)(2,1)} async-done(((bf16[512,256]{1,0:T(8,128)(2,1)}), bf16[8192,256]{1,0:T(8,128)(2,1)}) %all-gather.2.cloned.1.call-update) | async-done | bytes 4194320 | tf_op jit(solution)/shard_map/all_gather | solution.py:51
  78.0 31.7 %convolution_convert_fusion = bf16[256,8192]{1,0:T(8,128)(2,1)} fusion(bf16[1024,8192]{1,0:T(8,128)(2,1)} %param.4, f32[1024,256]{1,0:T(8,128)} %param.5, bf16[8192,256]{1,0:T(8,128)(2,1)} %all-gather.2.cloned.1.call-done), kind=kOutput, calls=%fused_computation | convolution fusion | flops 8592556032 | bytes 26214400 | tf_op jit(solution)/shard_map/dot_general | solution.py:57
  109.7 2.6 %copy.21 = bf16[32,16,8,512]{3,2,0,1:T(8,128)(2,1)S(1)} copy(bf16[32,16,8,512]{3,2,1,0:T(8,128)(2,1)} %bitcast.59) | data formatting | bytes 8388608 | tf_op jit(solution)/shard_map/reshape | solution.py:19
  112.3 55.3 %all_to_all.30 = bf16[16,512,256]{1,2,0:T(8,128)(2,1)} all-to-all(bf16[16,512,256]{1,2,0:T(8,128)(2,1)S(1)} %bitcast.58), channel_id=1, replica_groups=mesh['dp_0'=2,'dp_1'=4,'dp_2'=2,'mp_0'=2,'mp_1'=4] {'dp_0','dp_1','dp_2'}, dimensions={0} | all-to-all | bytes 8388608 | tf_op jit(solution)/shard_map/all_to_all | solution.py:25
  167.7 2.8 %reduce_sum.39 = bf16[512,256]{0,1:T(8,128)(2,1)S(1)} reduce(bf16[16,512,256]{1,2,0:T(8,128)(2,1)} %all_to_all.30, bf16[]{:T(256)} %constant.6.clone.1), dimensions={0}, to_apply=%region_0.0 | reduce | flops 1966080 | bytes 4456450 | tf_op jit(solution)/shard_map/reduce_sum | solution.py:26
  170.5 0.9 copy.13
  171.4 5.3 %all-to-all-start.2 = ((bf16[512,1,2,128]{3,2,1,0:T(2,128)(2,1)}), bf16[512,1,2,128]{3,2,1,0:T(2,128)(2,1)S(1)}, u32[]{:S(2)}, u32[]{:S(2)}) async-start(bf16[512,1,2,128]{3,2,1,0:T(2,128)(2,1)} %copy.13), calls=%async_computation.2 | async-start | bytes 524288 | tf_op jit(solution)/shard_map/all_to_all | solution.py:63
  176.7 14.3 %convolution_multiply_fusion.1 = f32[12,12]{1,0:T(8,128)S(1)} fusion(f32[12,131072]{1,0:T(8,128)} %param.6), kind=kOutput, calls=%fused_computation.4 | convolution fusion | flops 226492560 | bytes 6292032 | tf_op jit(solution)/shard_map/dot_general | solution.py:75
  190.9 0.0 all-to-all-done.2
  191.0 0.4 copy.15
  191.4 11.4 %fusion.2 = f32[12]{0:T(128)S(1)} fusion(f32[131072,1]{0,1:T(1,128)S(1)} %bitcast.60, f32[12,131072]{1,0:T(8,128)} %param.6), kind=kOutput, calls=%fused_computation.8 | convolution fusion | flops 18874380 | bytes 6815792 | tf_op jit(solution)/shard_map/dot_general | solution.py:73
  202.9 0.7 multiply_reduce_fusion
  204.3 7.1 %all-reduce.4 = (f32[12]{0:T(128)S(1)}, f32[]{:T(128)}, f32[12,12]{1,0:T(8,128)S(1)}) all-reduce(f32[12]{0:T(128)S(1)} %fusion.2, f32[]{:T(128)S(6)} %div.36, f32[12,12]{1,0:T(8,128)S(1)} %convolution_multiply_fusion.1), channel_id=1, replica_groups=mesh['dp_0'=2,'dp_1'=4,'dp_2'=2,'mp_0'=2,'mp_1'=4] {'dp_0'}, use_global_device_ids=true, to_apply=%region_1.0 | all-reduce | flops 157 | bytes 1256 | tf_op jit(solution)/shard_map/psum | solution.py:30
  211.3 8.7 %all-reduce.1 = (f32[12]{0:T(128)S(1)}, f32[]{:T(128)}, f32[12,12]{1,0:T(8,128)S(1)}) all-reduce(f32[12]{0:T(128)S(1)} %get-tuple-element.14, f32[]{:T(128)} %get-tuple-element.15, f32[12,12]{1,0:T(8,128)S(1)} %get-tuple-element.16), channel_id=1, replica_groups=mesh['dp_0'=2,'dp_1'=4,'dp_2'=2,'mp_0'=2,'mp_1'=4] {'dp_1'}, use_global_device_ids=true, to_apply=%region_2.0 | all-reduce | flops 157 | bytes 1256 | tf_op jit(solution)/shard_map/psum | solution.py:30
  220.0 3.1 %all-reduce.3 = (f32[12]{0:T(128)S(1)}, f32[]{:T(128)}, f32[12,12]{1,0:T(8,128)S(1)}) all-reduce(f32[12]{0:T(128)S(1)} %get-tuple-element.5, f32[]{:T(128)} %get-tuple-element.6, f32[12,12]{1,0:T(8,128)S(1)} %get-tuple-element.7), channel_id=1, replica_groups=mesh['dp_0'=2,'dp_1'=4,'dp_2'=2,'mp_0'=2,'mp_1'=4] {'dp_2'}, use_global_device_ids=true, to_apply=%region_3.0 | all-reduce | flops 157 | bytes 1256 | tf_op jit(solution)/shard_map/psum | solution.py:30
  223.1 5.7 %all-reduce.2 = (f32[12]{0:T(128)S(1)}, f32[]{:T(128)}, f32[12,12]{1,0:T(8,128)S(1)}) all-reduce(f32[12]{0:T(128)S(1)} %get-tuple-element.11, f32[]{:T(128)} %get-tuple-element.12, f32[12,12]{1,0:T(8,128)S(1)} %get-tuple-element.13), channel_id=1, replica_groups=mesh['dp_0'=2,'dp_1'=4,'dp_2'=2,'mp_0'=2,'mp_1'=4] {'mp_0'}, use_global_device_ids=true, to_apply=%region_4.0 | all-reduce | flops 157 | bytes 1256 | tf_op jit(solution)/shard_map/psum | solution.py:30
  228.8 11.7 %all-reduce = (f32[12]{0:T(128)S(1)}, f32[]{:T(128)}, f32[12,12]{1,0:T(8,128)S(1)}) all-reduce(f32[12]{0:T(128)S(1)} %get-tuple-element.8, f32[]{:T(128)} %get-tuple-element.9, f32[12,12]{1,0:T(8,128)S(1)} %get-tuple-element.10), channel_id=1, replica_groups=mesh['dp_0'=2,'dp_1'=4,'dp_2'=2,'mp_0'=2,'mp_1'=4] {'mp_1'}, use_global_device_ids=true, to_apply=%region_5.0 | all-reduce | flops 157 | bytes 1256 | tf_op jit(solution)/shard_map/psum | solution.py:30
  240.4 0.6 multiply_reduce_fusion.1
  241.0 6.4 %fusion.5 = f32[1,131072]{1,0:T(1,128)S(1)} fusion(f32[12,131072]{1,0:T(8,128)} %param.6, f32[12]{0:T(128)S(1)} %get-tuple-element.2), kind=kOutput, calls=%fused_computation.16 | convolution fusion | flops 18874368 | bytes 6815792 | tf_op jit(solution)/shard_map/dot_general | solution.py:77
  247.4 0.8 fusion.3
  250.3 0.6 pad_maximum_fusion
  250.9 0.8 subtract_divide_fusion
  (1 shorter events, 0.0 us)
Async XLA Ops:
  7.2 70.8 %all-gather.2.cloned.1.call-start = ((), (), s32[]{:S(2)}) async-start(), calls=%async_computation.3 | async-start | bytes 4456448 | tf_op jit(solution)/shard_map/all_gather | solution.py:51
  171.4 19.6 %all-to-all-start.2 = ((bf16[512,1,2,128]{3,2,1,0:T(2,128)(2,1)}), bf16[512,1,2,128]{3,2,1,0:T(2,128)(2,1)S(1)}, u32[]{:S(2)}, u32[]{:S(2)}) async-start(bf16[512,1,2,128]{3,2,1,0:T(2,128)(2,1)} %copy.13), calls=%async_computation.2 | async-start | bytes 524288 | tf_op jit(solution)/shard_map/all_to_all | solution.py:63
Sparse Core Ops, SparseCore 0:
  22.8 55.1 all-gather.1
where the time goes:
time: 259 us
  blocking collectives  105 us (41%)
  matrix products  64.6 us (25%)
  waiting for transfers between devices  55.3 us (21%)
  between operations  16.8 us (6%)
  other arithmetic  6.73 us (3%)
  starting transfers between devices  5.34 us (2%)
  local copies, waits for them, and re-layouts  4.83 us (2%)
    all_to_all x1, blocking collectives, summed_on_arrival(): lax.all_to_all(tiles, axis, split_axis=0, concat_axis=0, tiled=True)  55.3 us
    all_gather x1, waiting for transfers between devices, body(): lax.all_gather(local_rows, DP, axis=0, tiled=True)  55.3 us
    psum x5, blocking collectives, over_axes(): return functools.reduce(lax.psum, axes, value)  36.2 us
    dot_general x1, matrix products, body(): lax.dot_general(columns, weighted, (((0,), (0,)), ((), ())), preferred_el...  31.7 us
    dot_general x1, matrix products, body(): jnp.dot(basis, basis.T, precision=lax.Precision.HIGHEST) / param_total  14.3 us
    all_to_all x1, blocking collectives, body(): lax.all_to_all(lowered_duplicate, MP, split_axis=1, concat_axis=0, tiled=...  13.5 us
    dot_general x1, matrix products, body(): jnp.dot(basis, curved, precision=lax.Precision.HIGHEST) / param_total  11.4 us
    dot_general x1, matrix products, body(): jnp.dot(coeffs, basis, precision=lax.Precision.HIGHEST)  6.4 us
  transfers between devices with their start and end apart: 2, of which 1 were waited for; matrix products, arithmetic and copies ran while one was open for 6% of the time, Pallas kernels for 0%

commit v1 on v0

v1 whole, which is shorter than its diff:
```python
import jax
import jax.numpy as jnp
from jax import lax
from jax.experimental import pallas as pl
from jax.experimental.pallas import tpu as pltpu
from jax.sharding import PartitionSpec as P

MESH = pl.DeviceIdType.MESH
TOKENS = 16384
PARAMS = 16777216
NB = 12
F32 = jnp.float32
BF16 = jnp.bfloat16
BLK = 256


def kernel(
    act_hbm, curv_hbm, basis_hbm, kry_ref, out_ref, hess_ref,
    act, curv, basis, vmat, ksend, zoth, acc, wt,
    dsend, drecv, xfs, xns, xfr, xl, xr, ysend, yrecv, zsend, zrecv, curved,
    arz, ary, arx,
    lsem, zs_s, zs_r, ys_s, ys_r, xr_s, xr_r, xl_s, xl_r, xf_s, xf_r, d_s, d_r,
    d2_s, d2_r, f2_s, f2_r, n2_s, l2_r, r2_r, y2_s, y2_r, z2_s, z2_r,
    az_s, az_r, ay_s, ay_r, ax_s, ax_r,
):
    dp = lax.axis_index("dp")
    mp = lax.axis_index("mp")
    c = lax.rem(dp, 2)
    x = lax.rem(dp // 2, 4)
    y = (dp // 8) * 2 + mp // 4
    yl = mp // 4
    z = lax.rem(mp, 4)
    oc = 1 - c

    def dev(xx, yy, zz, cc):
        return {"dp": ((yy // 2) * 4 + xx) * 2 + cc, "mp": lax.rem(yy, 2) * 4 + zz}

    def mod4(v):
        return lax.rem(v + 8, 4)

    def blk(xx, dy, cc):
        yy = mod4(y + dy)
        return (((yy // 2) * 4 + xx) * 2 + cc) * 2 + lax.rem(yy, 2)

    def rows(b):
        return pl.ds(pl.multiple_of(b * BLK, BLK), BLK)

    def rcopy(src, dst, ss, rs, device):
        return pltpu.make_async_remote_copy(
            src_ref=src, dst_ref=dst, send_sem=ss, recv_sem=rs, device_id=device, device_id_type=MESH
        )

    ld_basis = pltpu.make_async_copy(basis_hbm, basis, lsem.at[0])
    ld_act = pltpu.make_async_copy(act_hbm, act, lsem.at[1])
    ld_curv = pltpu.make_async_copy(curv_hbm, curv, lsem.at[2])
    ld_basis.start()
    ld_act.start()
    ld_curv.start()

    barrier = pltpu.get_barrier_semaphore()
    partners = [dev(x, y, z, oc)]
    for k in (1, 2, 3):
        partners.append(dev(x, y, mod4(z + k), c))
        partners.append(dev(x, y, mod4(z + k), oc))
        partners.append(dev(x, mod4(y + k), z, c))
        partners.append(dev(mod4(x + k), y, z, c))
    for p in partners:
        pl.semaphore_signal(barrier, inc=1, device_id=p, device_id_type=MESH)

    for h in range(8):
        for kv in range(2):
            v = kry_ref[pl.ds(2 * h + kv, 64, stride=16), :]
            ksend[h % 4, h // 4, :, kv * 128 : (kv + 1) * 128] = v.astype(BF16)
    b0 = blk(x, 0, c)
    zrow = pl.multiple_of(z * 64, 64)
    vrow = pl.multiple_of(b0 * BLK + z * 64, 64)
    vmat[pl.ds(vrow, 64), :] = ksend[z, yl]
    zoth[pl.ds(zrow, 64), :] = ksend[z, 1 - yl]
    acc[...] = jnp.zeros_like(acc)

    pl.semaphore_wait(barrier, len(partners))

    sends = []
    zrecvs = []
    for k in (2, 1, 3):
        zt = mod4(z + k)
        d = dev(x, y, zt, c)
        for q, (src, dst) in enumerate(
            (
                (ksend.at[zt, 1 - yl], zoth.at[pl.ds(zrow, 64), :]),
                (ksend.at[zt, yl], vmat.at[pl.ds(vrow, 64), :]),
            )
        ):
            cp = rcopy(src, dst, zs_s.at[q * 3 + k - 1], zs_r.at[q * 3 + k - 1], d)
            cp.start()
            sends.append(cp)
            zrecvs.append(cp)

    def gram_chunk(i, carry):
        top, bot = carry
        top, bot = list(top), list(bot)
        cols = pl.ds(pl.multiple_of(i * 128, 128), 128)
        a = basis[0:8, cols]
        b = basis[8:12, cols]
        for j in range(NB):
            row = a[j : j + 1] if j < 8 else b[j - 8 : j - 7]
            top[j] = top[j] + a * jnp.broadcast_to(row, (8, 128))
            bot[j] = bot[j] + b * jnp.broadcast_to(row, (4, 128))
        return tuple(top), tuple(bot)

    gram_state = (
        tuple(jnp.zeros((8, 128), F32) for _ in range(NB)),
        tuple(jnp.zeros((4, 128), F32) for _ in range(NB)),
    )

    ld_basis.wait()
    gram_state = lax.fori_loop(0, 1024, gram_chunk, gram_state)

    for cp in zrecvs:
        cp.wait_recv()

    def vblk(b):
        return vmat.at[rows(b), :]

    def mm1(b):
        def tile(m, _):
            r = pl.ds(pl.multiple_of(m * 256, 256), 256)
            acc[r, :] += jnp.dot(act[r, rows(b)], vmat[rows(b), :], preferred_element_type=F32)
            return 0

        lax.fori_loop(0, 4, tile, 0)

    xp, xm, xf = mod4(x + 1), mod4(x - 1), mod4(x + 2)

    def x_right(dy):
        b = blk(x, dy, c)
        return rcopy(vblk(b), vblk(b), xr_s.at[dy], xr_r.at[dy], dev(xp, y, z, c))

    def x_left(dy):
        b = blk(x, dy, c)
        return rcopy(vblk(b), vblk(b), xl_s.at[dy], xl_r.at[dy], dev(xm, y, z, c))

    def x_far(dy):
        odd = lax.rem(dy, 2)
        b = blk(mod4(x - 1 + 2 * odd), dy, c)
        return rcopy(vblk(b), vblk(b), xf_s.at[dy], xf_r.at[dy], dev(mod4(x + 1 - 2 * odd), y, z, c))

    def d2d(xo, dy):
        b = blk(mod4(x + xo), dy, c)
        return rcopy(vblk(b), vblk(b), d_s.at[xo * 4 + dy], d_r.at[xo * 4 + dy], dev(x, y, z, oc))

    def to_dy(i):
        return i + (i // 2) * (5 - 2 * i)

    ycps = {}
    for k in (2, 1, 3):
        src = vblk(b0) if k == 2 else zoth
        cp = rcopy(src, vblk(b0), ys_s.at[k], ys_r.at[4 - k], dev(x, mod4(y + k), z, c))
        cp.start()
        sends.append(cp)
        ycps[4 - k] = cp
    ld_act.wait()
    for i in range(4):
        dy = (0, 1, 3, 2)[i]
        if dy:
            ycps[dy].wait_recv()
        x_right(dy).start()
        x_left(dy).start()
        d2d(0, dy).start()
        mm1(blk(x, dy, c))

    def near(i, _):
        dy = to_dy(i)
        x_right(dy).wait_recv()
        d2d(3, dy).start()
        x_left(dy).wait_recv()
        x_far(dy).start()
        d2d(1, dy).start()
        mm1(blk(xm, dy, c))
        mm1(blk(xp, dy, c))
        d2d(0, dy).wait_recv()
        mm1(blk(x, dy, oc))
        return 0

    lax.fori_loop(0, 4, near, 0)

    def far(i, _):
        dy = to_dy(i)
        x_far(dy).wait_recv()
        d2d(2, dy).start()
        mm1(blk(xf, dy, c))
        for xo, xx in ((3, xm), (1, xp)):
            d2d(xo, dy).wait_recv()
            mm1(blk(xx, dy, oc))
        return 0

    lax.fori_loop(0, 4, far, 0)

    def last(i, _):
        dy = to_dy(i)
        d2d(2, dy).wait_recv()
        mm1(blk(xf, dy, oc))
        return 0

    lax.fori_loop(0, 4, last, 0)

    ld_curv.wait()
    for m in range(4):
        r = slice(m * 256, (m + 1) * 256)
        wt[:, r] = (curv[r, :] * acc[r, :]).T.astype(BF16)

    def mm2(b):
        return jnp.dot(wt[...], act[:, rows(b)], preferred_element_type=F32)

    def d2d2(i):
        return rcopy(dsend.at[i], drecv.at[i], d2_s.at[i], d2_r.at[i], dev(x, y, z, oc))

    def xo_of(i):
        return i

    def idx(xo, dy):
        return xo * 4 + dy

    def other(i, _):
        g = i // 4
        xo = lax.rem(2 + g * 3, 4)
        k = xo * 4 + lax.rem(i, 4)
        dsend[k] = mm2(blk(mod4(x + xo), lax.rem(i, 4), oc)).astype(BF16)
        d2d2(k).start()
        return 0

    lax.fori_loop(0, 16, other, 0)

    def chip_sum(xo, dy):
        k = idx(xo, dy)
        own = mm2(blk(mod4(x + xo), dy, c))
        d2d2(k).wait_recv()
        return own + drecv[k].astype(F32)

    def far2(dy):
        odd = lax.rem(dy, 2)
        return rcopy(xfs.at[dy], xfr.at[dy], f2_s.at[dy], f2_r.at[dy], dev(mod4(x - 1 + 2 * odd), y, z, c))

    def right2(dy):
        return rcopy(xns.at[dy], xl.at[dy], n2_s.at[dy], l2_r.at[dy], dev(xp, y, z, c))

    def left2(dy):
        return rcopy(xns.at[4 + dy], xr.at[dy], n2_s.at[4 + dy], r2_r.at[dy], dev(xm, y, z, c))

    def far_send(i, _):
        dy = to_dy(3 - i)
        xfs[dy] = chip_sum(2, dy).astype(BF16)
        far2(dy).start()
        return 0

    lax.fori_loop(0, 4, far_send, 0)

    def near_send(i, _):
        dy = to_dy(3 - i)
        odd = lax.rem(dy, 2)
        xo = 1 + 2 * odd
        xns[odd * 4 + dy] = chip_sum(xo, dy).astype(BF16)

        @pl.when(odd == 0)
        def _():
            right2(dy).start()

        @pl.when(odd == 1)
        def _():
            left2(dy).start()

        return 0

    lax.fori_loop(0, 4, near_send, 0)

    def near_add(i, _):
        dy = to_dy(3 - i)
        odd = lax.rem(dy, 2)
        xo = 3 - 2 * odd
        s = chip_sum(xo, dy)
        far2(dy).wait_recv()
        xns[(1 - odd) * 4 + dy] = (s + xfr[dy].astype(F32)).astype(BF16)

        @pl.when(odd == 0)
        def _():
            left2(dy).start()

        @pl.when(odd == 1)
        def _():
            right2(dy).start()

        return 0

    lax.fori_loop(0, 4, near_add, 0)

    def x_sum(dy):
        s = chip_sum(0, dy)
        right2(dy).wait_recv()
        left2(dy).wait_recv()
        return s + xl[dy].astype(F32) + xr[dy].astype(F32)

    def y2(k):
        return rcopy(ysend.at[k], yrecv.at[4 - k], y2_s.at[k], y2_r.at[4 - k], dev(x, mod4(y + k), z, c))

    for k in (2, 3, 1):
        ysend[k] = x_sum(k).astype(BF16)
        cp = y2(k)
        cp.start()
        sends.append(cp)
    h_own = x_sum(0)
    y2(1).wait_recv()
    y2(3).wait_recv()
    h_oth = yrecv[1].astype(F32) + yrecv[3].astype(F32)
    h_oth = h_oth.T.astype(BF16)
    for zz in range(4):
        zsend[zz, 1 - yl] = h_oth[zz * 64 : (zz + 1) * 64, :]
    y2(2).wait_recv()
    h_own = (h_own + yrecv[2].astype(F32)).T.astype(BF16)
    for zz in range(4):
        zsend[zz, yl] = h_own[zz * 64 : (zz + 1) * 64, :]

    zcps = []
    for k in (2, 1, 3):
        zt = mod4(z + k)
        cp = rcopy(zsend.at[zt], zrecv.at[z], z2_s.at[k - 1], z2_r.at[k - 1], dev(x, y, zt, c))
        cp.start()
        sends.append(cp)
        zcps.append(cp)
    zrecv[z] = zsend[z]
    for cp in zcps:
        cp.wait_recv()

    for zz in range(4):
        for hl in range(2):
            for kv in range(2):
                v = zrecv[zz, hl, :, kv * 128 : (kv + 1) * 128].astype(F32) * (1.0 / TOKENS)
                curved[pl.ds(2 * (hl * 4 + zz) + kv, 64, stride=16), :] = v

    def dot_chunk(i, carry):
        tops, bots, sq = carry
        tops, bots = list(tops), list(bots)
        t = curved[pl.ds(pl.multiple_of(i * 8, 8), 8), :]
        for s in range(8):
            cols = pl.ds(pl.multiple_of(i * 1024 + s * 128, 128), 128)
            row = t[s : s + 1]
            tops[s % 4] = tops[s % 4] + basis[0:8, cols] * jnp.broadcast_to(row, (8, 128))
            bots[s % 4] = bots[s % 4] + basis[8:12, cols] * jnp.broadcast_to(row, (4, 128))
        return tuple(tops), tuple(bots), sq + t * t

    tops, bots, sq = lax.fori_loop(
        0,
        128,
        dot_chunk,
        (
            tuple(jnp.zeros((8, 128), F32) for _ in range(4)),
            tuple(jnp.zeros((4, 128), F32) for _ in range(4)),
            jnp.zeros((8, 128), F32),
        ),
    )
    top = (tops[0] + tops[1]) + (tops[2] + tops[3])
    bot = (bots[0] + bots[1]) + (bots[2] + bots[3])

    lane8 = lax.broadcasted_iota(jnp.int32, (8, 128), 1)
    sub8 = lax.broadcasted_iota(jnp.int32, (8, 128), 0)
    zero4 = jnp.zeros((4, 128), F32)

    def lanes(v):
        return jnp.broadcast_to(jnp.sum(v, axis=1, keepdims=True), (8, 128))

    def pad(v):
        return jnp.concatenate([v, zero4], axis=0)

    up = jnp.where(lane8 == NB, lanes(top), 0.0)
    dn = jnp.where(lane8 == NB, lanes(pad(bot)), 0.0)
    for j in range(NB):
        up = jnp.where(lane8 == j, lanes(gram_state[0][j]), up)
        dn = jnp.where(lane8 == j, lanes(pad(gram_state[1][j])), dn)
    up = jnp.where(lane8 == NB + 1, lanes(sq), up)

    me = z * 2 + c
    arz[me, 0:8, :] = up
    arz[me, 8:16, :] = dn
    cps = []
    for k in range(1, 8):
        t = lax.rem(me + k, 8)
        cp = rcopy(
            arz.at[me], arz.at[me], az_s.at[k], az_r.at[k], dev(x, y, t // 2, lax.rem(t, 2))
        )
        cp.start()
        cps.append(cp)
    for cp in cps:
        cp.wait_recv()
    sends += cps
    tot = arz[0]
    for k in range(1, 8):
        tot = tot + arz[k]
    for buf, me, ss, rs, axis in ((ary, y, ay_s, ay_r, 0), (arx, x, ax_s, ax_r, 1)):
        buf[me] = tot
        cps = []
        for k in (2, 1, 3):
            t = mod4(me + k)
            d = dev(x, t, z, c) if axis == 0 else dev(t, y, z, c)
            cp = rcopy(buf.at[me], buf.at[me], ss.at[k], rs.at[k], d)
            cp.start()
            cps.append(cp)
        for cp in cps:
            cp.wait_recv()
        sends += cps
        tot = (buf[0] + buf[1]) + (buf[2] + buf[3])

    tot = tot * (1.0 / PARAMS)
    gt, gb = tot[0:8], tot[8:16]

    def pick(v, lane):
        return lanes(jnp.where(lane8 == lane, v, 0.0))

    ct, cb = pick(gt, NB), pick(gb, NB)
    crow = jnp.sum(
        jnp.where(lane8 == sub8, ct, 0.0) + jnp.where(lane8 == sub8 + 8, cb, 0.0), axis=0, keepdims=True
    )
    gc = jnp.sum(gt * ct + gb * cb, axis=0, keepdims=True)
    cgc = jnp.sum(crow * gc, axis=1, keepdims=True)
    cc = jnp.sum(crow * crow, axis=1, keepdims=True)
    squares = jnp.sum(jnp.where(lane8 == NB + 1, gt, 0.0), axis=0, keepdims=True)
    squares = jnp.sum(squares, axis=1, keepdims=True)
    norm = jnp.sqrt(squares - 2.0 * cc + cgc + 1e-06)
    inv = jnp.broadcast_to(1.0 / norm, (8, 128))
    lane1 = lax.broadcasted_iota(jnp.int32, (1, 128), 1)
    hess_ref[...] = jnp.where(lane1 == NB, jnp.broadcast_to(norm, (1, 128)), crow)

    def res_chunk(i, _):
        t = []
        for s in range(8):
            cols = pl.ds(pl.multiple_of(i * 1024 + s * 128, 128), 128)
            t.append(basis[0:8, cols] * ct + pad(basis[8:12, cols]) * cb)
        for sh in (4, 2, 1):
            keep = lax.rem(sub8 // sh, 2) == 0
            t = [
                jnp.where(
                    keep,
                    t[s] + pltpu.roll(t[s], 8 - sh, 0),
                    t[s + sh] + pltpu.roll(t[s + sh], sh, 0),
                )
                for s in range(sh)
            ]
        r = pl.ds(pl.multiple_of(i * 8, 8), 8)
        out_ref[r, :] = (curved[r, :] - t[0]) * inv
        return 0

    lax.fori_loop(0, 128, res_chunk, 0)

    for cp in sends:
        cp.wait_send()

    def drain(dy, _):
        x_right(dy).wait_send()
        x_left(dy).wait_send()
        x_far(dy).wait_send()
        far2(dy).wait_send()
        right2(dy).wait_send()
        left2(dy).wait_send()
        for xo in range(4):
            d2d(xo, dy).wait_send()
            d2d2(xo * 4 + dy).wait_send()
        return 0

    lax.fori_loop(0, 4, drain, 0)


def body(activations, curvature, basis, krylov):
    dma = pltpu.SemaphoreType.DMA
    vm = pltpu.VMEM
    anyspace = pl.BlockSpec(memory_space=pl.ANY)
    vspace = pl.BlockSpec(memory_space=pltpu.VMEM)
    blocks = lambda n: vm((n, 256, 256), BF16)
    out, hess = pl.pallas_call(
        kernel,
        out_shape=(jax.ShapeDtypeStruct((1024, 128), F32), jax.ShapeDtypeStruct((1, 128), F32)),
        in_specs=[anyspace, anyspace, anyspace, vspace],
        out_specs=(vspace, vspace),
        scratch_shapes=[
            vm((1024, 8192), BF16),
            vm((1024, 256), F32),
            vm((NB, 131072), F32),
            vm((8192, 256), BF16),
            vm((4, 2, 64, 256), BF16),
            vm((256, 256), BF16),
            vm((1024, 256), F32),
            vm((256, 1024), BF16),
            blocks(16),
            blocks(16),
            blocks(4),
            blocks(8),
            blocks(4),
            blocks(4),
            blocks(4),
            blocks(4),
            blocks(4),
            vm((4, 2, 64, 256), BF16),
            vm((4, 2, 64, 256), BF16),
            vm((1024, 128), F32),
            vm((8, 16, 128), F32),
            vm((4, 16, 128), F32),
            vm((4, 16, 128), F32),
            dma((3,)),
            dma((6,)),
            dma((6,)),
            dma((4,)),
            dma((4,)),
            dma((4,)),
            dma((4,)),
            dma((4,)),
            dma((4,)),
            dma((4,)),
            dma((4,)),
            dma((16,)),
            dma((16,)),
            dma((16,)),
            dma((16,)),
            dma((4,)),
            dma((4,)),
            dma((8,)),
            dma((4,)),
            dma((4,)),
            dma((4,)),
            dma((4,)),
            dma((3,)),
            dma((3,)),
            dma((8,)),
            dma((8,)),
            dma((4,)),
            dma((4,)),
            dma((4,)),
            dma((4,)),
        ],
        compiler_params=pltpu.CompilerParams(
            collective_id=0, has_side_effects=True, vmem_limit_bytes=63 * 1024 * 1024
        ),
    )(activations, curvature, basis, krylov.reshape(1024, 128))
    return out.reshape(131072), hess[0, :13]


def solution(mesh):
    placed = (P("dp", None), P("dp", "mp"), P(None, ("dp", "mp")), P(("dp", "mp")))
    return jax.shard_map(
        body, mesh=mesh, in_specs=placed, out_specs=(P(("dp", "mp")), P()), check_vma=False
    )
```

time: 259 us -> 115 us (0.44)
  Pallas kernels: 0 us -> 111 us
  blocking collectives: 105 us -> 0 us
  matrix products: 64.6 us -> 0 us
  waiting for transfers between devices: 55.3 us -> 0 us
  between operations: 16.8 us -> 0.64 us
  other arithmetic: 6.73 us -> 0 us
  starting transfers between devices: 5.34 us -> 0 us
    pallas_call x0 -> x1, Pallas kernels: none -> 111 us  [body(): pl.pallas_call(kernel, out_shape=(jax.ShapeDtypeStruct((1024, 128), F32),...]
    all_to_all x2 -> x0, blocking collectives: 68.8 us -> none  [the longest x1 55.3 us: summed_on_arrival(): lax.all_to_all(tiles, axis, split_axis=0, concat_axis=0, tiled=True)]
    dot_general x5 -> x0, matrix products: 64.6 us -> none  [the longest x1 31.7 us: body(): lax.dot_general(columns, weighted, (((0,), (0,)), ((), ())), preferred_el...]
    all_gather x1 -> x0, waiting for transfers between devices: 55.3 us -> none  [body(): lax.all_gather(local_rows, DP, axis=0, tiled=True)]
    psum x5 -> x0, blocking collectives: 36.2 us -> none  [over_axes(): return functools.reduce(lax.psum, axes, value)]
    all_to_all x1 -> x0, starting transfers between devices: 5.3 us -> none  [body(): lax.all_to_all(scattered.reshape(rows_dev * model_count, local_heads, 2,...]
    reduce_sum x3 -> x0, other arithmetic: 4.19 us -> none  [the longest x1 2.84 us: summed_on_arrival(): return arrived.astype(jnp.float32).sum(axis=0)]
    reshape x2 -> x0, local copies, waits for them, and re-layouts: 2.81 us -> none  [the longest x1 2.63 us: in_blocks(): value.reshape(*shape[:dim], peers, shape[dim] // peers, *shape[dim + 1:])]
  transfers between devices with their start and end apart: 2 -> 0, of which waited for: 1 -> 0; matrix products, arithmetic and copies ran while one was open for 6% -> 0% of each run, Pallas kernels for 0% -> 0%
where the time goes in v1:
time: 115 us; the launch traced here: 114 us
  Pallas kernels  111 us (97%)
  local copies, waits for them, and re-layouts  2.97 us (3%)
    pallas_call x1, Pallas kernels, body(): pl.pallas_call(kernel, out_shape=(jax.ShapeDtypeStruct((1024, 128), F32),...  111 us

profile of v1, /device:TPU:0, one launch (start us, length us, event | category | flops | bytes accessed | tf_op | source)
XLA Modules:
  0.0 114.5 jit_solution(11135566307622865)
XLA Ops:
  0.6 110.9 %shard_map.59 = (f32[1024,128]{1,0:T(8,128)}, f32[1,128]{1,0:T(1,128)}) custom-call(bf16[1024,8192]{1,0:T(8,128)(2,1)} %act_hbm.1, f32[1024,256]{1,0:T(8,128)} %curv_hbm.1, f32[12,131072]{1,0:T(8,128)} %basis_hbm.1, f32[1024,128]{1,0:T(8,128)} %bitcast.4), custom_call_target="tpu_custom_call" | custom-call | tf_op jit(solution)/shard_map/pallas_call | solution.py:476
  111.5 1.1 slice_bitcast_fusion
  112.6 1.9 %copy.7 = f32[131072]{0:T(1024)} copy(f32[131072]{0:T(1024)} %bitcast.5) | data formatting | bytes 1048576

commit v2 on v1

v2 whole, which is shorter than its diff:
```python
import functools

import jax
import jax.numpy as jnp
from jax import lax
from jax.experimental import pallas as pl
from jax.experimental.pallas import tpu as pltpu
from jax.sharding import PartitionSpec as P

MESH = pl.DeviceIdType.MESH
TOKENS = 16384
PARAMS = 16777216
NB = 12
F32 = jnp.float32
BF16 = jnp.bfloat16
GRAM_UNROLL = 4
VMEM_MIB = 46
GRAM_PIECES = 8
BLK = 256


def kernel(
    act_hbm, curv, basis_hbm, kry_ref, out_ref, hess_ref,
    act, basis, vmat, ksend, zoth, acc, wt,
    dsend, drecv, xfs, xns, xfr, xl, xr, ysend, yrecv, zsend, zrecv, curved,
    arz, ary, arx, crz, cry, crx,
    lsem, zs_s, zs_r, ys_s, ys_r, xr_s, xr_r, xl_s, xl_r, xf_s, xf_r, d_s, d_r,
    d2_s, d2_r, f2_s, f2_r, n2_s, l2_r, r2_r, y2_s, y2_r, z2_s, z2_r,
    az_s, az_r, ay_s, ay_r, ax_s, ax_r, cz_s, cz_r, cy_s, cy_r, cx_s, cx_r,
):
    dp = lax.axis_index("dp")
    mp = lax.axis_index("mp")
    c = lax.rem(dp, 2)
    x = lax.rem(dp // 2, 4)
    y = (dp // 8) * 2 + mp // 4
    yl = mp // 4
    z = lax.rem(mp, 4)
    oc = 1 - c

    def dev(xx, yy, zz, cc):
        return {"dp": ((yy // 2) * 4 + xx) * 2 + cc, "mp": lax.rem(yy, 2) * 4 + zz}

    def mod4(v):
        return lax.rem(v + 8, 4)

    def blk(xx, dy, cc):
        yy = mod4(y + dy)
        return (((yy // 2) * 4 + xx) * 2 + cc) * 2 + lax.rem(yy, 2)

    def rows(b):
        return pl.ds(pl.multiple_of(b * BLK, BLK), BLK)

    def rcopy(src, dst, ss, rs, device):
        return pltpu.make_async_remote_copy(
            src_ref=src, dst_ref=dst, send_sem=ss, recv_sem=rs, device_id=device, device_id_type=MESH
        )

    ld_basis = pltpu.make_async_copy(basis_hbm, basis, lsem.at[0])
    ld_act = pltpu.make_async_copy(act_hbm, act, lsem.at[1])
    ld_basis.start()
    ld_act.start()
    barrier = pltpu.get_barrier_semaphore()
    partners = [dev(x, y, z, oc)]
    for k in (1, 2, 3):
        partners.append(dev(x, y, mod4(z + k), c))
        partners.append(dev(x, y, mod4(z + k), oc))
        partners.append(dev(x, mod4(y + k), z, c))
        partners.append(dev(mod4(x + k), y, z, c))
    for p in partners:
        pl.semaphore_signal(barrier, inc=1, device_id=p, device_id_type=MESH)

    for h in range(8):
        for kv in range(2):
            v = kry_ref[pl.ds(2 * h + kv, 64, stride=16), :]
            ksend[h % 4, h // 4, :, kv * 128 : (kv + 1) * 128] = v.astype(BF16)
    b0 = blk(x, 0, c)
    zrow = pl.multiple_of(z * 64, 64)
    vrow = pl.multiple_of(b0 * BLK + z * 64, 64)
    vmat[pl.ds(vrow, 64), :] = ksend[z, yl]
    zoth[pl.ds(zrow, 64), :] = ksend[z, 1 - yl]
    acc[...] = jnp.zeros_like(acc)

    pl.semaphore_wait(barrier, len(partners))

    sends = []
    zrecvs = ([], [])
    for q in range(2):
        for k in (2, 1, 3):
            zt = mod4(z + k)
            if q == 0:
                src, dst = ksend.at[zt, 1 - yl], zoth.at[pl.ds(zrow, 64), :]
            else:
                src, dst = ksend.at[zt, yl], vmat.at[pl.ds(vrow, 64), :]
            n = q * 3 + k - 1
            cp = rcopy(src, dst, zs_s.at[n], zs_r.at[n], dev(x, y, zt, c))
            cp.start()
            sends.append(cp)
            zrecvs[q].append(cp)

    def gram_chunk(i, carry):
        top, bot = carry
        top, bot = list(top), list(bot)
        for u in range(GRAM_UNROLL):
            cols = pl.ds(pl.multiple_of(i * (128 * GRAM_UNROLL) + u * 128, 128), 128)
            a = basis[0:8, cols]
            b = basis[8:12, cols]
            for j in range(NB):
                row = a[j : j + 1] if j < 8 else b[j - 8 : j - 7]
                top[j] = top[j] + a * jnp.broadcast_to(row, (8, 128))
                bot[j] = bot[j] + b * jnp.broadcast_to(row, (4, 128))
        return tuple(top), tuple(bot)

    gram_state = [
        (
            tuple(jnp.zeros((8, 128), F32) for _ in range(NB)),
            tuple(jnp.zeros((4, 128), F32) for _ in range(NB)),
        )
    ]
    steps = 1024 // GRAM_UNROLL // GRAM_PIECES
    done = [0]

    def gram():
        n = done[0]
        gram_state[0] = lax.fori_loop(n * steps, (n + 1) * steps, gram_chunk, gram_state[0])
        done[0] = n + 1

    def vblk(b):
        return vmat.at[rows(b), :]

    def mm1(bs):
        for m in range(2):
            r = slice(m * 512, (m + 1) * 512)
            p = [jnp.dot(act[r, rows(b)], vmat[rows(b), :], preferred_element_type=F32) for b in bs]
            acc[r, :] += functools.reduce(jnp.add, p)

    xp, xm, xf = mod4(x + 1), mod4(x - 1), mod4(x + 2)

    def x_right(dy):
        b = blk(x, dy, c)
        return rcopy(vblk(b), vblk(b), xr_s.at[dy], xr_r.at[dy], dev(xp, y, z, c))

    def x_left(dy):
        b = blk(x, dy, c)
        return rcopy(vblk(b), vblk(b), xl_s.at[dy], xl_r.at[dy], dev(xm, y, z, c))

    def x_far(dy):
        odd = lax.rem(dy, 2)
        b = blk(mod4(x - 1 + 2 * odd), dy, c)
        return rcopy(vblk(b), vblk(b), xf_s.at[dy], xf_r.at[dy], dev(mod4(x + 1 - 2 * odd), y, z, c))

    def d2d(xo, dy):
        b = blk(mod4(x + xo), dy, c)
        return rcopy(vblk(b), vblk(b), d_s.at[xo * 4 + dy], d_r.at[xo * 4 + dy], dev(x, y, z, oc))

    def to_dy(i):
        return i + (i // 2) * (5 - 2 * i)

    ld_basis.wait()
    gram()

    ycps = {}

    def y_send(k):
        src = vblk(b0) if k == 2 else zoth
        cp = rcopy(src, vblk(b0), ys_s.at[k], ys_r.at[4 - k], dev(x, mod4(y + k), z, c))
        cp.start()
        sends.append(cp)
        ycps[4 - k] = cp

    def own_block(dy):
        x_right(dy).start()
        x_left(dy).start()
        d2d(0, dy).start()

    def ring(dy):
        x_right(dy).wait_recv()
        x_left(dy).wait_recv()
        x_far(dy).start()
        d2d(3, dy).start()
        d2d(1, dy).start()

    def mine(*which):
        mm1([blk(xx, dy, c) for xx, dy in which])

    def others(*which):
        for xo, dy in which:
            d2d(xo, dy).wait_recv()
        mm1([blk(mod4(x + xo), dy, oc) for xo, dy in which])

    for cp in zrecvs[0]:
        cp.wait_recv()
    y_send(1)
    y_send(3)
    for cp in zrecvs[1]:
        cp.wait_recv()
    own_block(0)
    y_send(2)
    gram()
    ld_act.wait()
    mine((x, 0))
    ycps[1].wait_recv()
    own_block(1)
    ycps[3].wait_recv()
    own_block(3)
    ring(0)
    gram()
    mine((x, 1), (x, 3))
    ring(1)
    mine((xm, 0), (xp, 0))
    ycps[2].wait_recv()
    own_block(2)
    gram()
    others((0, 0), (0, 1))
    ring(3)
    mine((xm, 1), (xp, 1))
    gram()
    ring(2)
    mine((x, 2))
    gram()
    others((0, 3), (3, 0), (1, 0))
    x_far(0).wait_recv()
    d2d(2, 0).start()
    mine((xm, 3), (xp, 3), (xm, 2), (xp, 2))
    x_far(1).wait_recv()
    d2d(2, 1).start()
    gram()
    mine((xf, 0), (xf, 1))
    others((3, 1), (1, 1), (0, 2), (2, 0))
    x_far(3).wait_recv()
    d2d(2, 3).start()
    mine((xf, 3))
    gram()
    others((3, 3), (1, 3), (3, 2), (1, 2), (2, 1))
    x_far(2).wait_recv()
    d2d(2, 2).start()
    mine((xf, 2))
    others((2, 3), (2, 2))
    gram_state = gram_state[0]

    lane8 = lax.broadcasted_iota(jnp.int32, (8, 128), 1)
    sub8 = lax.broadcasted_iota(jnp.int32, (8, 128), 0)
    zero4 = jnp.zeros((4, 128), F32)

    def lanes(v):
        return jnp.broadcast_to(jnp.sum(v, axis=1, keepdims=True), (8, 128))

    def pad(v):
        return jnp.concatenate([v, zero4], axis=0)

    def reduce_start(stage, buf, value, ss, rs):
        me, count = ((z * 2 + c, 8), (y, 4), (x, 4))[stage]
        buf[me] = value
        cps = []
        for k in range(1, count):
            t = lax.rem(me + k, count)
            d = (
                dev(x, y, t // 2, lax.rem(t, 2)) if stage == 0 else dev(x, t, z, c) if stage == 1 else dev(t, y, z, c)
            )
            cp = rcopy(buf.at[me], buf.at[me], ss.at[k], rs.at[k], d)
            cp.start()
            cps.append(cp)
        sends.extend(cps)
        return cps, buf, count

    def reduce_end(started):
        cps, buf, count = started
        for cp in cps:
            cp.wait_recv()
        parts = [buf[k] for k in range(count)]
        while len(parts) > 1:
            parts = [parts[k] + parts[k + 1] for k in range(0, len(parts), 2)]
        return parts[0]

    gup = jnp.zeros((8, 128), F32)
    gdn = jnp.zeros((8, 128), F32)
    for j in range(NB):
        gup = jnp.where(lane8 == j, lanes(gram_state[0][j]), gup)
        gdn = jnp.where(lane8 == j, lanes(pad(gram_state[1][j])), gdn)
    gram_sum = reduce_start(0, arz, jnp.concatenate([gup, gdn], axis=0), az_s, az_r)


    for m in range(4):
        r = slice(m * 256, (m + 1) * 256)
        wt[:, r] = (curv[r, :] * acc[r, :]).T.astype(BF16)

    def mm2(b):
        return jnp.dot(wt[...], act[:, rows(b)], preferred_element_type=F32)

    def d2d2(i):
        return rcopy(dsend.at[i], drecv.at[i], d2_s.at[i], d2_r.at[i], dev(x, y, z, oc))

    def idx(xo, dy):
        return xo * 4 + dy

    def other(*which):
        ps = [mm2(blk(mod4(x + xo), dy, oc)).astype(BF16) for xo, dy in which]
        for (xo, dy), p in zip(which, ps):
            dsend[idx(xo, dy)] = p
        for xo, dy in which:
            d2d2(idx(xo, dy)).start()

    def chip_sums(*which):
        ps = [mm2(blk(mod4(x + xo), dy, c)) for xo, dy in which]
        for xo, dy in which:
            d2d2(idx(xo, dy)).wait_recv()
        return [p + drecv[idx(xo, dy)].astype(F32) for (xo, dy), p in zip(which, ps)]

    def far2(dy):
        odd = lax.rem(dy, 2)
        return rcopy(xfs.at[dy], xfr.at[dy], f2_s.at[dy], f2_r.at[dy], dev(mod4(x - 1 + 2 * odd), y, z, c))

    def right2(dy):
        return rcopy(xns.at[dy], xl.at[dy], n2_s.at[dy], l2_r.at[dy], dev(xp, y, z, c))

    def left2(dy):
        return rcopy(xns.at[4 + dy], xr.at[dy], n2_s.at[4 + dy], r2_r.at[dy], dev(xm, y, z, c))

    def far_send(*dys):
        for dy, s in zip(dys, chip_sums(*((2, dy) for dy in dys))):
            xfs[dy] = s.astype(BF16)
        for dy in dys:
            far2(dy).start()

    def near_send(*dys):
        for dy, s in zip(dys, chip_sums(*((1 + 2 * (dy % 2), dy) for dy in dys))):
            xns[(dy % 2) * 4 + dy] = s.astype(BF16)
        for dy in dys:
            (left2 if dy % 2 else right2)(dy).start()

    def near_add(*dys):
        sums = chip_sums(*((3 - 2 * (dy % 2), dy) for dy in dys))
        for dy in dys:
            far2(dy).wait_recv()
        for dy, s in zip(dys, sums):
            xns[(1 - dy % 2) * 4 + dy] = (s + xfr[dy].astype(F32)).astype(BF16)
        for dy in dys:
            (right2 if dy % 2 else left2)(dy).start()

    early, late = (2, 3), (1, 0)
    other((2, 2), (2, 3))
    other((2, 1), (2, 0))
    other((1, 2), (3, 3))
    far_send(*early)
    far_send(*late)
    other((3, 1), (1, 0))
    near_send(*early)
    other((3, 2), (1, 3))
    near_send(*late)
    other((1, 1), (3, 0))
    gram_sum = reduce_start(1, ary, reduce_end(gram_sum), ay_s, ay_r)
    near_add(*early)
    other((0, 2), (0, 3))
    near_add(*late)
    other((0, 1), (0, 0))
    gram_sum = reduce_start(2, arx, reduce_end(gram_sum), ax_s, ax_r)
    x_own = dict(zip((2, 3, 1, 0), chip_sums((0, 2), (0, 3), (0, 1), (0, 0))))

    def x_sum(dy):
        right2(dy).wait_recv()
        left2(dy).wait_recv()
        return x_own[dy] + xl[dy].astype(F32) + xr[dy].astype(F32)

    def y2(k):
        return rcopy(ysend.at[k], yrecv.at[4 - k], y2_s.at[k], y2_r.at[4 - k], dev(x, mod4(y + k), z, c))

    for k in (2, 3, 1):
        ysend[k] = x_sum(k).astype(BF16)
        cp = y2(k)
        cp.start()
        sends.append(cp)
    h_own = x_sum(0)
    y2(1).wait_recv()
    y2(3).wait_recv()
    h_oth = yrecv[1].astype(F32) + yrecv[3].astype(F32)
    zcps = []

    def z2(value, head, q):
        v = value.T.astype(BF16)
        for zz in range(4):
            zsend[zz, head] = v[zz * 64 : (zz + 1) * 64, :]
        for k in (2, 1, 3):
            zt = mod4(z + k)
            n = q * 3 + k - 1
            cp = rcopy(zsend.at[zt, head], zrecv.at[z, head], z2_s.at[n], z2_r.at[n], dev(x, y, zt, c))
            cp.start()
            sends.append(cp)
            zcps.append(cp)

    z2(h_oth, 1 - yl, 0)
    y2(2).wait_recv()
    z2(h_own + yrecv[2].astype(F32), yl, 1)
    zrecv[z] = zsend[z]
    for cp in zcps:
        cp.wait_recv()

    for zz in range(4):
        for hl in range(2):
            for kv in range(2):
                v = zrecv[zz, hl, :, kv * 128 : (kv + 1) * 128].astype(F32) * (1.0 / TOKENS)
                curved[pl.ds(2 * (hl * 4 + zz) + kv, 64, stride=16), :] = v

    def dot_chunk(i, carry):
        tops, bots, sq = carry
        tops, bots = list(tops), list(bots)
        for u in range(4):
            t = curved[pl.ds(pl.multiple_of(i * 32 + u * 8, 8), 8), :]
            sq = sq + t * t
            for s in range(8):
                cols = pl.ds(pl.multiple_of(i * 4096 + u * 1024 + s * 128, 128), 128)
                row = t[s : s + 1]
                tops[s % 4] = tops[s % 4] + basis[0:8, cols] * jnp.broadcast_to(row, (8, 128))
                bots[s % 4] = bots[s % 4] + basis[8:12, cols] * jnp.broadcast_to(row, (4, 128))
        return tuple(tops), tuple(bots), sq

    tops, bots, sq = lax.fori_loop(
        0,
        32,
        dot_chunk,
        (
            tuple(jnp.zeros((8, 128), F32) for _ in range(4)),
            tuple(jnp.zeros((4, 128), F32) for _ in range(4)),
            jnp.zeros((8, 128), F32),
        ),
    )
    top = (tops[0] + tops[1]) + (tops[2] + tops[3])
    bot = (bots[0] + bots[1]) + (bots[2] + bots[3])

    row = jnp.sum(
        jnp.where(lane8 == sub8, lanes(top), 0.0)
        + jnp.where(lane8 == sub8 + 8, lanes(pad(bot)), 0.0)
        + jnp.where(lane8 == NB, lanes(sq), 0.0),
        axis=0,
        keepdims=True,
    )
    row = reduce_end(reduce_start(0, crz, row, cz_s, cz_r))
    row = reduce_end(reduce_start(1, cry, row, cy_s, cy_r))
    row = reduce_end(reduce_start(2, crx, row, cx_s, cx_r))
    row = row * (1.0 / PARAMS)
    tot = reduce_end(gram_sum) * (1.0 / PARAMS)
    gt, gb = tot[0:8], tot[8:16]
    lane1 = lax.broadcasted_iota(jnp.int32, (1, 128), 1)
    crow = jnp.where(lane1 < NB, row, 0.0)
    ct = lanes(jnp.where(lane8 == sub8, jnp.broadcast_to(crow, (8, 128)), 0.0))
    cb = lanes(jnp.where(lane8 == sub8 + 8, jnp.broadcast_to(crow, (8, 128)), 0.0))
    gc = jnp.sum(gt * ct + gb * cb, axis=0, keepdims=True)
    cgc = jnp.sum(crow * gc, axis=1, keepdims=True)
    cc = jnp.sum(crow * crow, axis=1, keepdims=True)
    squares = jnp.sum(jnp.where(lane1 == NB, row, 0.0), axis=1, keepdims=True)
    norm = jnp.sqrt(squares - 2.0 * cc + cgc + 1e-06)
    inv = jnp.broadcast_to(1.0 / norm, (8, 128))
    hess_ref[...] = jnp.where(lane1 == NB, jnp.broadcast_to(norm, (1, 128)), crow)

    def res_chunk(i, _):
        for u in range(4):
            t = []
            for s in range(8):
                cols = pl.ds(pl.multiple_of(i * 4096 + u * 1024 + s * 128, 128), 128)
                t.append(basis[0:8, cols] * ct + pad(basis[8:12, cols]) * cb)
            for sh in (4, 2, 1):
                keep = lax.rem(sub8 // sh, 2) == 0
                t = [
                    jnp.where(
                        keep,
                        t[s] + pltpu.roll(t[s], 8 - sh, 0),
                        t[s + sh] + pltpu.roll(t[s + sh], sh, 0),
                    )
                    for s in range(sh)
                ]
            r = pl.ds(pl.multiple_of(i * 32 + u * 8, 8), 8)
            out_ref[r, :] = (curved[r, :] - t[0]) * inv
        return 0

    lax.fori_loop(0, 32, res_chunk, 0)

    for cp in sends:
        cp.wait_send()

    def drain(dy, _):
        x_right(dy).wait_send()
        x_left(dy).wait_send()
        x_far(dy).wait_send()
        far2(dy).wait_send()
        right2(dy).wait_send()
        left2(dy).wait_send()
        for xo in range(4):
            d2d(xo, dy).wait_send()
            d2d2(xo * 4 + dy).wait_send()
        return 0

    lax.fori_loop(0, 4, drain, 0)


def body(activations, curvature, basis, krylov):
    dma = pltpu.SemaphoreType.DMA
    vm = pltpu.VMEM
    anyspace = pl.BlockSpec(memory_space=pltpu.HBM)
    vspace = pl.BlockSpec(memory_space=pltpu.VMEM)
    blocks = lambda n: vm((n, 256, 256), BF16)
    out, hess = pl.pallas_call(
        kernel,
        out_shape=(jax.ShapeDtypeStruct((1024, 128), F32), jax.ShapeDtypeStruct((1, 128), F32)),
        in_specs=[anyspace, vspace, anyspace, vspace],
        out_specs=(vspace, vspace),
        scratch_shapes=[
            vm((1024, 8192), BF16),
            vm((NB, 131072), F32),
            vm((8192, 256), BF16),
            vm((4, 2, 64, 256), BF16),
            vm((256, 256), BF16),
            vm((1024, 256), F32),
            vm((256, 1024), BF16),
            blocks(16),
            blocks(16),
            blocks(4),
            blocks(8),
            blocks(4),
            blocks(4),
            blocks(4),
            blocks(4),
            blocks(4),
            vm((4, 2, 64, 256), BF16),
            vm((4, 2, 64, 256), BF16),
            vm((1024, 128), F32),
            vm((8, 16, 128), F32),
            vm((4, 16, 128), F32),
            vm((4, 16, 128), F32),
            vm((8, 1, 128), F32),
            vm((4, 1, 128), F32),
            vm((4, 1, 128), F32),
            dma((3,)),
            dma((6,)),
            dma((6,)),
            dma((4,)),
            dma((4,)),
            dma((4,)),
            dma((4,)),
            dma((4,)),
            dma((4,)),
            dma((4,)),
            dma((4,)),
            dma((16,)),
            dma((16,)),
            dma((16,)),
            dma((16,)),
            dma((4,)),
            dma((4,)),
            dma((8,)),
            dma((4,)),
            dma((4,)),
            dma((4,)),
            dma((4,)),
            dma((6,)),
            dma((6,)),
            dma((8,)),
            dma((8,)),
            dma((4,)),
            dma((4,)),
            dma((4,)),
            dma((4,)),
            dma((8,)),
            dma((8,)),
            dma((4,)),
            dma((4,)),
            dma((4,)),
            dma((4,)),
        ],
        compiler_params=pltpu.CompilerParams(
            collective_id=0, has_side_effects=True, vmem_limit_bytes=VMEM_MIB * 1024 * 1024
        ),
    )(activations, curvature, basis, krylov.reshape(1024, 128))
    return out.reshape(131072), hess[0, :13]


def solution(mesh):
    placed = (P("dp", None), P("dp", "mp"), P(None, ("dp", "mp")), P(("dp", "mp")))
    return jax.shard_map(
        body, mesh=mesh, in_specs=placed, out_specs=(P(("dp", "mp")), P()), check_vma=False
    )
```

time: 115 us -> 87.7 us (0.76)
  Pallas kernels: 111 us -> 83.3 us
    pallas_call x1, Pallas kernels: 111 us -> 83.3 us  [body(): pl.pallas_call(kernel, out_shape=(jax.ShapeDtypeStruct((1024, 128), F32),...]
    unnamed x1 -> x5, local copies, waits for them, and re-layouts: 1.87 us -> 3.09 us
where the time goes in v2:
time: 87.7 us; the launch traced here: 87.5 us
  Pallas kernels  83.3 us (95%)
  local copies, waits for them, and re-layouts  3.6 us (4%)
    pallas_call x1, Pallas kernels, body(): pl.pallas_call(kernel, out_shape=(jax.ShapeDtypeStruct((1024, 128), F32),...  83.3 us
    unnamed x5, local copies, waits for them, and re-layouts  3.09 us

profile of v2, /device:TPU:0, one launch (start us, length us, event | category | flops | bytes accessed | tf_op | source)
XLA Modules:
  0.0 87.5 jit_solution(12258777860344220699)
XLA Ops:
  0.6 0.0 copy-start
  0.6 1.2 %copy-done = f32[1024,256]{1,0:T(8,128)S(1)} copy-done((f32[1024,256]{1,0:T(8,128)S(1)}, f32[1024,256]{1,0:T(8,128)}, u32[]{:S(2)}) %copy-start) | copy-done | bytes 1048600
  1.9 0.0 copy-start.1
  1.9 1.0 %copy-done.1 = f32[131072]{0:T(1024)S(1)} copy-done((f32[131072]{0:T(1024)S(1)}, f32[131072]{0:T(1024)}, u32[]{:S(2)}) %copy-start.1) | copy-done | bytes 524312
  2.9 83.3 %shard_map.59 = (f32[1024,128]{1,0:T(8,128)S(1)}, f32[1,128]{1,0:T(1,128)S(1)}) custom-call(bf16[1024,8192]{1,0:T(8,128)(2,1)} %act_hbm.1, f32[1024,256]{1,0:T(8,128)S(1)} %copy-done, f32[12,131072]{1,0:T(8,128)} %basis_hbm.1, f32[1024,128]{1,0:T(8,128)S(1)} %bitcast.4), custom_call_target="tpu_custom_call" | custom-call | tf_op jit(solution)/shard_map/pallas_call | solution.py:499
  86.2 0.5 slice_bitcast_fusion
  86.7 0.8 copy.7
Async XLA Ops:
  0.6 1.2 %copy-start = (f32[1024,256]{1,0:T(8,128)S(1)}, f32[1024,256]{1,0:T(8,128)}, u32[]{:S(2)}) copy-start(f32[1024,256]{1,0:T(8,128)} %curv.1) | copy-start | bytes 3145732
  1.9 1.0 %copy-start.1 = (f32[131072]{0:T(1024)S(1)}, f32[131072]{0:T(1024)}, u32[]{:S(2)}) copy-start(f32[131072]{0:T(1024)} %param.7) | copy-start | bytes 1572868

commit v3 on v2

--- a/solution.py
+++ b/solution.py
@@ -14,14 +14,14 @@
 F32 = jnp.float32
 BF16 = jnp.bfloat16
 GRAM_UNROLL = 4
-VMEM_MIB = 46
+VMEM_BYTES = 55_750_000
 GRAM_PIECES = 8
 BLK = 256
 
 
 def kernel(
-    act_hbm, curv, basis_hbm, kry_ref, out_ref, hess_ref,
-    act, basis, vmat, ksend, zoth, acc, wt,
+    act_hbm, curv_hbm, basis_hbm, kry_hbm, out_ref, hess_ref,
+    act, curv, basis, kry_ref, vmat, ksend, zoth, acc, wt,
     dsend, drecv, xfs, xns, xfr, xl, xr, ysend, yrecv, zsend, zrecv, curved,
     arz, ary, arx, crz, cry, crx,
     lsem, zs_s, zs_r, ys_s, ys_r, xr_s, xr_r, xl_s, xl_r, xf_s, xf_r, d_s, d_r,
@@ -55,10 +55,18 @@
             src_ref=src, dst_ref=dst, send_sem=ss, recv_sem=rs, device_id=device, device_id_type=MESH
         )
 
-    ld_basis = pltpu.make_async_copy(basis_hbm, basis, lsem.at[0])
+    first, rest = pl.ds(0, 32768), pl.ds(32768, 98304)
+    ld_basis = pltpu.make_async_copy(basis_hbm.at[:, first], basis.at[:, first], lsem.at[0])
+    ld_rest = pltpu.make_async_copy(basis_hbm.at[:, rest], basis.at[:, rest], lsem.at[4])
     ld_act = pltpu.make_async_copy(act_hbm, act, lsem.at[1])
+    ld_curv = pltpu.make_async_copy(curv_hbm, curv, lsem.at[2])
+    ld_kry = pltpu.make_async_copy(kry_hbm, kry_ref, lsem.at[3])
+    ld_kry.start()
     ld_basis.start()
     ld_act.start()
+    ld_rest.start()
+    ld_curv.start()
+
     barrier = pltpu.get_barrier_semaphore()
     partners = [dev(x, y, z, oc)]
     for k in (1, 2, 3):
@@ -69,6 +77,9 @@
     for p in partners:
         pl.semaphore_signal(barrier, inc=1, device_id=p, device_id_type=MESH)
 
+    acc[...] = jnp.zeros_like(acc)
+    ld_kry.wait()
+
     for h in range(8):
         for kv in range(2):
             v = kry_ref[pl.ds(2 * h + kv, 64, stride=16), :]
@@ -78,7 +89,6 @@
     vrow = pl.multiple_of(b0 * BLK + z * 64, 64)
     vmat[pl.ds(vrow, 64), :] = ksend[z, yl]
     zoth[pl.ds(zrow, 64), :] = ksend[z, 1 - yl]
-    acc[...] = jnp.zeros_like(acc)
 
     pl.semaphore_wait(barrier, len(partners))
 
@@ -157,6 +167,7 @@
 
     ld_basis.wait()
     gram()
+    gram()
 
     ycps = {}
 
@@ -195,9 +206,10 @@
         cp.wait_recv()
     own_block(0)
     y_send(2)
-    gram()
     ld_act.wait()
     mine((x, 0))
+    ld_rest.wait()
+    gram()
     ycps[1].wait_recv()
     own_block(1)
     ycps[3].wait_recv()
@@ -209,27 +221,27 @@
     mine((xm, 0), (xp, 0))
     ycps[2].wait_recv()
     own_block(2)
-    gram()
-    others((0, 0), (0, 1))
+    mine((xm, 1), (xp, 1))
     ring(3)
-    mine((xm, 1), (xp, 1))
-    gram()
+    gram()
+    gram()
+    others((0, 0), (0, 1), (0, 3))
+    gram()
+    others((3, 0), (1, 0))
+    mine((x, 2), (xm, 3), (xp, 3))
     ring(2)
-    mine((x, 2))
-    gram()
-    others((0, 3), (3, 0), (1, 0))
+    mine((xm, 2), (xp, 2))
     x_far(0).wait_recv()
     d2d(2, 0).start()
-    mine((xm, 3), (xp, 3), (xm, 2), (xp, 2))
+    mine((xf, 0))
+    gram()
     x_far(1).wait_recv()
     d2d(2, 1).start()
-    gram()
-    mine((xf, 0), (xf, 1))
+    mine((xf, 1))
     others((3, 1), (1, 1), (0, 2), (2, 0))
     x_far(3).wait_recv()
     d2d(2, 3).start()
     mine((xf, 3))
-    gram()
     others((3, 3), (1, 3), (3, 2), (1, 2), (2, 1))
     x_far(2).wait_recv()
     d2d(2, 2).start()
@@ -278,6 +290,7 @@
         gdn = jnp.where(lane8 == j, lanes(pad(gram_state[1][j])), gdn)
     gram_sum = reduce_start(0, arz, jnp.concatenate([gup, gdn], axis=0), az_s, az_r)
 
+    ld_curv.wait()
 
     for m in range(4):
         r = slice(m * 256, (m + 1) * 256)
@@ -345,12 +358,14 @@
     other((3, 1), (1, 0))
     near_send(*early)
     other((3, 2), (1, 3))
-    near_send(*late)
+    near_send(1)
     other((1, 1), (3, 0))
     gram_sum = reduce_start(1, ary, reduce_end(gram_sum), ay_s, ay_r)
     near_add(*early)
     other((0, 2), (0, 3))
-    near_add(*late)
+    near_add(1)
+    near_send(0)
+    near_add(0)
     other((0, 1), (0, 0))
     gram_sum = reduce_start(2, arx, reduce_end(gram_sum), ax_s, ax_r)
     x_own = dict(zip((2, 3, 1, 0), chip_sums((0, 2), (0, 3), (0, 1), (0, 0))))
@@ -499,11 +514,13 @@
     out, hess = pl.pallas_call(
         kernel,
         out_shape=(jax.ShapeDtypeStruct((1024, 128), F32), jax.ShapeDtypeStruct((1, 128), F32)),
-        in_specs=[anyspace, vspace, anyspace, vspace],
+        in_specs=[anyspace] * 4,
         out_specs=(vspace, vspace),
         scratch_shapes=[
             vm((1024, 8192), BF16),
+            vm((1024, 256), F32),
             vm((NB, 131072), F32),
+            vm((1024, 128), F32),
             vm((8192, 256), BF16),
             vm((4, 2, 64, 256), BF16),
             vm((256, 256), BF16),
@@ -527,7 +544,7 @@
             vm((8, 1, 128), F32),
             vm((4, 1, 128), F32),
             vm((4, 1, 128), F32),
-            dma((3,)),
+            dma((5,)),
             dma((6,)),
             dma((6,)),
             dma((4,)),
@@ -565,7 +582,7 @@
             dma((4,)),
         ],
         compiler_params=pltpu.CompilerParams(
-            collective_id=0, has_side_effects=True, vmem_limit_bytes=VMEM_MIB * 1024 * 1024
+            collective_id=0, has_side_effects=True, vmem_limit_bytes=VMEM_BYTES
         ),
     )(activations, curvature, basis, krylov.reshape(1024, 128))
     return out.reshape(131072), hess[0, :13]

time: 87.7 us -> 83.4 us (0.951)
  local copies, waits for them, and re-layouts: 3.6 us -> 1.34 us
  Pallas kernels: 83.3 us -> 81.3 us
    unnamed x5 -> x1, local copies, waits for them, and re-layouts: 3.09 us -> 0.83 us
    pallas_call x1, Pallas kernels: 83.3 us -> 81.3 us  [body(): pl.pallas_call(kernel, out_shape=(jax.ShapeDtypeStruct((1024, 128), F32),...]
where the time goes in v3:
time: 83.4 us; the launch traced here: 83.3 us
  Pallas kernels  81.3 us (97%)
  local copies, waits for them, and re-layouts  1.34 us (2%)
    pallas_call x1, Pallas kernels, body(): pl.pallas_call(kernel, out_shape=(jax.ShapeDtypeStruct((1024, 128), F32),...  81.3 us

profile of v3, /device:TPU:0, one launch (start us, length us, event | category | flops | bytes accessed | tf_op | source)
XLA Modules:
  0.0 83.3 jit_solution(17433743587750464762)
XLA Ops:
  0.6 81.3 %shard_map.59 = (f32[1024,128]{1,0:T(8,128)S(1)}, f32[1,128]{1,0:T(1,128)S(1)}) custom-call(bf16[1024,8192]{1,0:T(8,128)(2,1)} %act_hbm.1, f32[1024,256]{1,0:T(8,128)} %curv_hbm.1, f32[12,131072]{1,0:T(8,128)} %basis_hbm.1, f32[1024,128]{1,0:T(8,128)} %bitcast.5), custom_call_target="tpu_custom_call" | custom-call | tf_op jit(solution)/shard_map/pallas_call | solution.py:514
  81.9 0.5 slice_bitcast_fusion
  82.4 0.8 copy.7

commit v4 on v3

--- a/solution.py
+++ b/solution.py
@@ -23,10 +23,10 @@
     act_hbm, curv_hbm, basis_hbm, kry_hbm, out_ref, hess_ref,
     act, curv, basis, kry_ref, vmat, ksend, zoth, acc, wt,
     dsend, drecv, xfs, xns, xfr, xl, xr, ysend, yrecv, zsend, zrecv, curved,
-    arz, ary, arx, crz, cry, crx,
+    yfs, yfr, arz, ary, arx, crz, cry, crx,
     lsem, zs_s, zs_r, ys_s, ys_r, xr_s, xr_r, xl_s, xl_r, xf_s, xf_r, d_s, d_r,
     d2_s, d2_r, f2_s, f2_r, n2_s, l2_r, r2_r, y2_s, y2_r, z2_s, z2_r,
-    az_s, az_r, ay_s, ay_r, ax_s, ax_r, cz_s, cz_r, cy_s, cy_r, cx_s, cx_r,
+    az_s, az_r, ay_s, ay_r, ax_s, ax_r, cz_s, cz_r, cy_s, cy_r, cx_s, cx_r, yf_s, yf_r,
 ):
     dp = lax.axis_index("dp")
     mp = lax.axis_index("mp")
@@ -149,6 +149,8 @@
         b = blk(x, dy, c)
         return rcopy(vblk(b), vblk(b), xr_s.at[dy], xr_r.at[dy], dev(xp, y, z, c))
 
+    yf = dev(x, mod4(y + 2), z, c)
+
     def x_left(dy):
         b = blk(x, dy, c)
         return rcopy(vblk(b), vblk(b), xl_s.at[dy], xl_r.at[dy], dev(xm, y, z, c))
@@ -330,50 +332,65 @@
 
     def far_send(*dys):
         for dy, s in zip(dys, chip_sums(*((2, dy) for dy in dys))):
+            if dy == 0:
+                y_far(0).wait_recv()
+                s = s + yfr[0].astype(F32)
             xfs[dy] = s.astype(BF16)
         for dy in dys:
             far2(dy).start()
 
     def near_send(*dys):
         for dy, s in zip(dys, chip_sums(*((1 + 2 * (dy % 2), dy) for dy in dys))):
+            if dy == 0:
+                y_far(1).wait_recv()
+                s = s + yfr[1].astype(F32)
             xns[(dy % 2) * 4 + dy] = s.astype(BF16)
         for dy in dys:
             (left2 if dy % 2 else right2)(dy).start()
 
     def near_add(*dys):
         sums = chip_sums(*((3 - 2 * (dy % 2), dy) for dy in dys))
-        for dy in dys:
-            far2(dy).wait_recv()
         for dy, s in zip(dys, sums):
-            xns[(1 - dy % 2) * 4 + dy] = (s + xfr[dy].astype(F32)).astype(BF16)
+            if dy != 2:
+                far2(dy).wait_recv()
+                s = s + xfr[dy].astype(F32)
+            xns[(1 - dy % 2) * 4 + dy] = s.astype(BF16)
         for dy in dys:
             (right2 if dy % 2 else left2)(dy).start()
 
-    early, late = (2, 3), (1, 0)
-    other((2, 2), (2, 3))
-    other((2, 1), (2, 0))
-    other((1, 2), (3, 3))
-    far_send(*early)
-    far_send(*late)
-    other((3, 1), (1, 0))
-    near_send(*early)
-    other((3, 2), (1, 3))
-    near_send(1)
-    other((1, 1), (3, 0))
+    def y_far(n):
+        return rcopy(yfs.at[n], yfr.at[n], yf_s.at[n], yf_r.at[n], yf)
+
+    other((2, 2), (1, 2))
+    other((2, 3), (2, 1))
+    other((3, 3), (3, 1))
+    for n, s in enumerate(chip_sums((2, 2), (1, 2))):
+        yfs[n] = s.astype(BF16)
+        y_far(n).start()
+    far_send(3, 1)
+    near_send(3, 1)
+    other((2, 0), (1, 3))
+    other((3, 2), (1, 1))
+    far_send(0)
+    near_add(3)
+    near_add(2)
+    other((1, 0), (3, 0))
+    near_add(1)
+    other((0, 2), (0, 3))
     gram_sum = reduce_start(1, ary, reduce_end(gram_sum), ay_s, ay_r)
-    near_add(*early)
-    other((0, 2), (0, 3))
-    near_add(1)
     near_send(0)
-    near_add(0)
     other((0, 1), (0, 0))
     gram_sum = reduce_start(2, arx, reduce_end(gram_sum), ax_s, ax_r)
     x_own = dict(zip((2, 3, 1, 0), chip_sums((0, 2), (0, 3), (0, 1), (0, 0))))
+    near_add(0)
 
     def x_sum(dy):
-        right2(dy).wait_recv()
         left2(dy).wait_recv()
-        return x_own[dy] + xl[dy].astype(F32) + xr[dy].astype(F32)
+        s = x_own[dy] + xr[dy].astype(F32)
+        if dy != 2:
+            right2(dy).wait_recv()
+            s = s + xl[dy].astype(F32)
+        return s
 
     def y2(k):
         return rcopy(ysend.at[k], yrecv.at[4 - k], y2_s.at[k], y2_r.at[4 - k], dev(x, mod4(y + k), z, c))
@@ -490,19 +507,19 @@
     for cp in sends:
         cp.wait_send()
 
-    def drain(dy, _):
+    for dy in range(4):
         x_right(dy).wait_send()
         x_left(dy).wait_send()
         x_far(dy).wait_send()
-        far2(dy).wait_send()
-        right2(dy).wait_send()
         left2(dy).wait_send()
+        if dy != 2:
+            far2(dy).wait_send()
+            right2(dy).wait_send()
         for xo in range(4):
             d2d(xo, dy).wait_send()
             d2d2(xo * 4 + dy).wait_send()
-        return 0
-
-    lax.fori_loop(0, 4, drain, 0)
+    for n in range(2):
+        y_far(n).wait_send()
 
 
 def body(activations, curvature, basis, krylov):
@@ -538,6 +555,8 @@
             vm((4, 2, 64, 256), BF16),
             vm((4, 2, 64, 256), BF16),
             vm((1024, 128), F32),
+            blocks(2),
+            blocks(2),
             vm((8, 16, 128), F32),
             vm((4, 16, 128), F32),
             vm((4, 16, 128), F32),
@@ -580,6 +599,8 @@
             dma((4,)),
             dma((4,)),
             dma((4,)),
+            dma((2,)),
+            dma((2,)),
         ],
         compiler_params=pltpu.CompilerParams(
             collective_id=0, has_side_effects=True, vmem_limit_bytes=VMEM_BYTES

time: 83.4 us -> 81.8 us (0.981)
  Pallas kernels: 81.3 us -> 79.7 us
    pallas_call x1, Pallas kernels: 81.3 us -> 79.7 us  [body(): pl.pallas_call(kernel, out_shape=(jax.ShapeDtypeStruct((1024, 128), F32),...]
where the time goes in v4:
time: 81.8 us; the launch traced here: 81.7 us
  Pallas kernels  79.7 us (97%)
  local copies, waits for them, and re-layouts  1.34 us (2%)
    pallas_call x1, Pallas kernels, body(): pl.pallas_call(kernel, out_shape=(jax.ShapeDtypeStruct((1024, 128), F32),...  79.7 us

profile of v4, /device:TPU:0, one launch (start us, length us, event | category | flops | bytes accessed | tf_op | source)
XLA Modules:
  0.0 81.7 jit_solution(16192165171868765752)
XLA Ops:
  0.6 79.7 %shard_map.59 = (f32[1024,128]{1,0:T(8,128)S(1)}, f32[1,128]{1,0:T(1,128)S(1)}) custom-call(bf16[1024,8192]{1,0:T(8,128)(2,1)} %act_hbm.1, f32[1024,256]{1,0:T(8,128)} %curv_hbm.1, f32[12,131072]{1,0:T(8,128)} %basis_hbm.1, f32[1024,128]{1,0:T(8,128)} %bitcast.5), custom_call_target="tpu_custom_call" | custom-call | tf_op jit(solution)/shard_map/pallas_call | solution.py:531
  80.4 0.5 slice_bitcast_fusion
  80.9 0.8 %copy.7 = f32[131072]{0:T(1024)} copy(f32[131072]{0:T(1024)S(1)} %bitcast.4) | data formatting | bytes 1048576

commit v5 on v4

--- a/solution.py
+++ b/solution.py
@@ -382,8 +382,6 @@
     other((0, 1), (0, 0))
     gram_sum = reduce_start(2, arx, reduce_end(gram_sum), ax_s, ax_r)
     x_own = dict(zip((2, 3, 1, 0), chip_sums((0, 2), (0, 3), (0, 1), (0, 0))))
-    near_add(0)
-
     def x_sum(dy):
         left2(dy).wait_recv()
         s = x_own[dy] + xr[dy].astype(F32)
@@ -396,6 +394,8 @@
         return rcopy(ysend.at[k], yrecv.at[4 - k], y2_s.at[k], y2_r.at[4 - k], dev(x, mod4(y + k), z, c))
 
     for k in (2, 3, 1):
+        if k == 1:
+            near_add(0)
         ysend[k] = x_sum(k).astype(BF16)
         cp = y2(k)
         cp.start()

time: 81.8 us -> 81.8 us (level)
  no operation moved by 1% of the time
where the time goes in v5:
time: 81.8 us; the launch traced here: 81.7 us
  Pallas kernels  79.7 us (97%)
  local copies, waits for them, and re-layouts  1.34 us (2%)
    pallas_call x1, Pallas kernels, body(): pl.pallas_call(kernel, out_shape=(jax.ShapeDtypeStruct((1024, 128), F32),...  79.7 us

profile of v5, /device:TPU:0, one launch (start us, length us, event | category | flops | bytes accessed | tf_op | source)
XLA Modules:
  0.0 81.7 jit_solution(11899433449707257322)
XLA Ops:
  0.6 79.7 %shard_map.59 = (f32[1024,128]{1,0:T(8,128)S(1)}, f32[1,128]{1,0:T(1,128)S(1)}) custom-call(bf16[1024,8192]{1,0:T(8,128)(2,1)} %act_hbm.1, f32[1024,256]{1,0:T(8,128)} %curv_hbm.1, f32[12,131072]{1,0:T(8,128)} %basis_hbm.1, f32[1024,128]{1,0:T(8,128)} %bitcast.5), custom_call_target="tpu_custom_call" | custom-call | tf_op jit(solution)/shard_map/pallas_call | solution.py:531
  80.4 0.5 slice_bitcast_fusion
  80.9 0.8 %copy.7 = f32[131072]{0:T(1024)} copy(f32[131072]{0:T(1024)S(1)} %bitcast.4) | data formatting | bytes 1048576
